TPU v7x, 128 devices: a whole 4x4x4 slice. The times are simulated.
128 devices in a mesh: dp: 32 (over x, z, core), tensor: 4 (over y).
Axes of the slice: x: 4, y: 4, z: 4, core: 2. Of those that a mesh axis runs over, the one named last changes fastest.
Arguments:
- tokens: bfloat16 [2, 2048, 4096], P(None, 'dp', 'tensor'), may hold values from -6 to 6
- routes: int32 [2, 2048, 2], P(None, 'dp'), may hold values from 0 to 7, all different within a row; in each aligned block of 64 rows (0 to 63, 64 to 127, ..., all dimensions but the last counted through in order) at most 20 rows name the same one
- probs: float32 [2, 2048, 8], P(None, 'dp'), may hold values from 0 to 1, as said below
- w_gate: bfloat16 [32, 4096, 3584], P('dp', None, 'tensor'), may hold values from -0.09375 to 0.09375
- w_up: bfloat16 [32, 4096, 3584], P('dp', None, 'tensor'), may hold values from -0.09375 to 0.09375
- w_down: bfloat16 [32, 3584, 4096], P('dp', 'tensor'), may hold values from -0.046875 to 0.046875
Outputs:
- mixed: bfloat16 [2, 2048, 4096], P(None, 'dp', 'tensor')
- aux_loss: float32 [2, 8], replicated
Inputs may be any that keep to these rules, and one draw needn't show every extreme that they name: `routes`: in each aligned block of 64 rows (the rows of one index of dp in one micro-batch) no expert is named in more than 20 entries; the 2 experts of a row differ. `probs`: each row is positive and sums to one.
All inputs are finite; a program needn't handle non-finite values.
Results may differ from a plain program's by a relative error of at most 0.012.
Values may be sent and summed in bfloat16 or wider, within the bound.
A program may use at most 128 MiB of HBM per device.

v0:
```python
import jax
import jax.numpy as jnp
from jax import lax
from jax.sharding import PartitionSpec as P

MICRO = 2
CAP = 20


def together(arrays, axis):
    ravelled, at, gathered = (jnp.concatenate([a.reshape(-1) for a in arrays]), 0, [])
    subtotal = lax.psum(ravelled, axis)
    for a in arrays:
        gathered.append(subtotal[at : at + a.size].reshape(a.shape))
        at += a.size
    return tuple(gathered)


def slot_tables(route, prob):
    rows_count = route.shape[0]
    experts = prob.shape[-1]
    capacity = CAP
    flat = route.reshape(-1)
    onehot = (flat[:, None] == jnp.arange(experts, dtype=jnp.int32)[None, :]).astype(jnp.int32)
    before = jnp.cumsum(onehot, axis=0) - onehot
    place = jnp.sum(before * onehot, axis=1)
    slot = flat * capacity + place
    picked = jnp.take_along_axis(prob, route, axis=1)
    weights = picked / jnp.sum(picked, axis=1, keepdims=True)
    grid = (slot[:, None] == jnp.arange(experts * capacity, dtype=jnp.int32)[None, :]).astype(
        jnp.float32
    )
    grid = grid.reshape(rows_count, route.shape[1], experts * capacity)
    dispatch = jnp.sum(grid, axis=1).T.astype(jnp.bfloat16)
    combine = jnp.sum(grid * weights[:, :, None], axis=1)
    counts = jnp.sum(onehot, axis=0).astype(jnp.float32)
    return (dispatch, combine, counts)


def spread_slots(slots, experts, copies_per, capacity):
    width = slots.shape[-1]
    wide = jnp.broadcast_to(
        slots.reshape(experts, 1, capacity, width), (experts, copies_per, capacity, width)
    )
    return wide.reshape(experts * copies_per, capacity, width)


def local(tokens, routes, probs, w_gate, w_up, w_down):
    groups = lax.axis_size("dp")
    experts = probs.shape[-1]
    copies_per = groups // experts
    capacity = CAP
    gate_local = w_gate[0]
    up_local = w_up[0]
    down_local = w_down[0]
    rows_local = tokens.shape[1]
    total_rows = rows_local * groups
    top_count = routes.shape[-1]
    tables = [slot_tables(routes[index], probs[index]) for index in range(MICRO)]
    prob_local = [jnp.sum(probs[index], axis=0) for index in range(MICRO)]
    count_table, prob_table = together(
        (jnp.stack([tables[index][2] for index in range(MICRO)]), jnp.stack(prob_local)), "dp"
    )
    outputs = []
    loss_terms = []
    for micro_index in range(MICRO):
        dispatch, combine, counts = tables[micro_index]
        count_all = count_table[micro_index]
        prob_all = prob_table[micro_index]
        width_local = tokens.shape[2]
        slots = jnp.dot(dispatch, tokens[micro_index], preferred_element_type=jnp.float32).astype(
            jnp.bfloat16
        )
        arrived = lax.all_to_all(
            spread_slots(slots, experts, copies_per, capacity),
            "dp",
            split_axis=0,
            concat_axis=0,
            tiled=True,
        )
        piece = lax.all_gather(arrived, "tensor", axis=2, tiled=True)
        piece_rows = piece.reshape(-1, piece.shape[2])
        gate = jnp.dot(piece_rows, gate_local, preferred_element_type=jnp.float32)
        up = jnp.dot(piece_rows, up_local, preferred_element_type=jnp.float32)
        hidden = (jax.nn.silu(gate) * up).astype(jnp.bfloat16)
        part = jnp.dot(hidden, down_local, preferred_element_type=jnp.float32).astype(jnp.bfloat16)
        reduced = lax.psum_scatter(part, "tensor", scatter_dimension=1, tiled=True).astype(
            jnp.float32
        )
        returned = lax.all_to_all(
            reduced.reshape(groups, capacity, width_local).astype(jnp.bfloat16),
            "dp",
            split_axis=0,
            concat_axis=0,
            tiled=True,
        ).astype(jnp.float32)
        summed = jnp.sum(returned.reshape(experts, copies_per, capacity, width_local), axis=1)
        mixed = jnp.dot(
            combine,
            summed.reshape(experts * capacity, width_local),
            precision=lax.Precision.HIGHEST,
            preferred_element_type=jnp.float32,
        )
        outputs.append(mixed.astype(jnp.bfloat16))
        loss_terms.append(
            experts * (count_all / (total_rows * top_count)) * (prob_all / total_rows)
        )
    return (jnp.stack(outputs), jnp.stack(loss_terms))


def solution(mesh):
    in_specs = (
        P(None, "dp", "tensor"),
        P(None, "dp", None),
        P(None, "dp", None),
        P("dp", None, "tensor"),
        P("dp", None, "tensor"),
        P("dp", "tensor", None),
    )
    out_specs = (P(None, "dp", "tensor"), P())
    return jax.shard_map(local, mesh=mesh, in_specs=in_specs, out_specs=out_specs, check_vma=False)
```

profile of v0, /device:TPU:1, one launch (start us, length us, event | category | flops | bytes accessed | tf_op | source)
XLA Modules:
  0.0 393.9 jit_solution(13326397115779215763)
XLA Ops:
  7.9 0.7 bitcast_or_fusion.1
  10.4 0.9 slice_reduce_fusion.1
  11.5 1.0 gather_fusion
  13.0 1.0 gather_fusion.1
  15.0 32.2 %all_to_all.20 = bf16[32,20,1024]{2,1,0:T(8,128)(2,1)} all-to-all(bf16[32,20,1024]{2,1,0:T(8,128)(2,1)S(1)} %bitcast.97), channel_id=1, replica_groups=mesh['dp'=32,'tensor'=4] {'dp'}, dimensions={0} | all-to-all | bytes 2621440 | tf_op jit(solution)/shard_map/all_to_all | solution.py:74
  47.8 26.4 %all_to_all.21 = bf16[32,20,1024]{2,1,0:T(8,128)(2,1)} all-to-all(bf16[32,20,1024]{2,1,0:T(8,128)(2,1)S(1)} %bitcast.98), channel_id=1, replica_groups=mesh['dp'=32,'tensor'=4] {'dp'}, dimensions={0} | all-to-all | bytes 2621440 | tf_op jit(solution)/shard_map/all_to_all | solution.py:74
  74.2 36.0 %all-gather.5.cloned.1.call-done = bf16[32,20,4096]{2,1,0:T(8,128)(2,1)} async-done(((bf16[32,20,1024]{2,1,0:T(8,128)(2,1)}), bf16[32,20,4096]{2,1,0:T(8,128)(2,1)}) %all-gather.5.cloned.1.call-update) | async-done | bytes 5242896 | tf_op jit(solution)/shard_map/all_gather | solution.py:81
  110.3 7.8 %reshape.140 = bf16[640,4096]{1,0:T(8,128)(2,1)} reshape(bf16[32,20,4096]{2,1,0:T(8,128)(2,1)} %all-gather.5.cloned.1.call-done) | data formatting | bytes 10485760 | tf_op jit(solution)/shard_map/reshape | solution.py:82
  118.0 11.7 %fusion.8 = f32[640,896]{1,0:T(8,128)S(1)} fusion(bf16[640,4096]{1,0:T(8,128)(2,1)} %reshape.140, bf16[1,4096,896]{2,1,0:T(8,128)(2,1)} %param.11), kind=kOutput, calls=%fused_computation.10 | convolution fusion | flops 4697620480 | bytes 14876672 | tf_op jit(solution)/shard_map/dot_general | solution.py:83
  129.7 18.9 %fusion.15 = bf16[640,4096]{1,0:T(8,128)(2,1)} fusion(bf16[1,896,4096]{2,1,0:T(8,128)(2,1)} %param.13, f32[640,896]{1,0:T(8,128)S(1)} %fusion.8, bf16[640,4096]{1,0:T(8,128)(2,1)} %reshape.140, bf16[1,4096,896]{2,1,0:T(8,128)(2,1)} %param.12), kind=kOutput, calls=%fused_computation.15 | convolution fusion | flops 9401303040 | bytes 27459584 | tf_op jit(solution)/shard_map/dot_general | solution.py:86
  148.8 29.4 %all-gather.3.cloned.1.call-done = bf16[32,20,4096]{2,1,0:T(8,128)(2,1)} async-done(((bf16[32,20,1024]{2,1,0:T(8,128)(2,1)}), bf16[32,20,4096]{2,1,0:T(8,128)(2,1)}) %all-gather.3.cloned.1.call-update) | async-done | bytes 5242896 | tf_op jit(solution)/shard_map/all_gather | solution.py:81
  178.2 7.7 %reshape.135 = bf16[640,4096]{1,0:T(8,128)(2,1)} reshape(bf16[32,20,4096]{2,1,0:T(8,128)(2,1)} %all-gather.3.cloned.1.call-done) | data formatting | bytes 10485760 | tf_op jit(solution)/shard_map/reshape | solution.py:82
  185.9 11.6 %fusion.10 = f32[640,896]{1,0:T(8,128)S(1)} fusion(bf16[640,4096]{1,0:T(8,128)(2,1)} %reshape.135, bf16[1,4096,896]{2,1,0:T(8,128)(2,1)} %param.11), kind=kOutput, calls=%fused_computation.12 | convolution fusion | flops 4697620480 | bytes 14876672 | tf_op jit(solution)/shard_map/dot_general | solution.py:83
  197.5 18.9 %fusion.12 = bf16[640,4096]{1,0:T(8,128)(2,1)} fusion(bf16[1,896,4096]{2,1,0:T(8,128)(2,1)} %param.13, f32[640,896]{1,0:T(8,128)S(1)} %fusion.10, bf16[640,4096]{1,0:T(8,128)(2,1)} %reshape.135, bf16[1,4096,896]{2,1,0:T(8,128)(2,1)} %param.12), kind=kOutput, calls=%fused_computation.14 | convolution fusion | flops 9401303040 | bytes 27459584 | tf_op jit(solution)/shard_map/dot_general | solution.py:86
  216.4 20.4 %reduce-scatter.5.cloned.1.call-done = bf16[640,1024]{1,0:T(8,128)(2,1)} async-done(((bf16[640,4096]{1,0:T(8,128)(2,1)}), bf16[640,1024]{1,0:T(8,128)(2,1)}) %reduce-scatter.5.cloned.1.call-update) | async-done | bytes 1310736 | tf_op jit(solution)/shard_map/reduce_scatter | solution.py:87
  236.8 3.2 convert_element_type.98
  240.0 7.7 %all-to-all-start.3 = ((bf16[32,20,1024]{2,1,0:T(8,128)(2,1)}), bf16[32,20,1024]{2,1,0:T(8,128)(2,1)S(1)}, u32[]{:S(2)}, u32[]{:S(2)}) async-start(bf16[32,20,1024]{2,1,0:T(8,128)(2,1)} %convert_element_type.98), calls=%async_computation.5 | async-start | bytes 3145728 | tf_op jit(solution)/shard_map/all_to_all | solution.py:90
  247.7 46.5 %reduce-scatter.3.cloned.1.call-done = bf16[640,1024]{1,0:T(8,128)(2,1)} async-done(((bf16[640,4096]{1,0:T(8,128)(2,1)}), bf16[640,1024]{1,0:T(8,128)(2,1)}) %reduce-scatter.3.cloned.1.call-update) | async-done | bytes 1310736 | tf_op jit(solution)/shard_map/reduce_scatter | solution.py:87
  294.3 3.2 convert_element_type.90
  297.5 7.7 %all-to-all-start.1 = ((bf16[32,20,1024]{2,1,0:T(8,128)(2,1)}), bf16[32,20,1024]{2,1,0:T(8,128)(2,1)S(1)}, u32[]{:S(2)}, u32[]{:S(2)}) async-start(bf16[32,20,1024]{2,1,0:T(8,128)(2,1)} %convert_element_type.90), calls=%async_computation.2 | async-start | bytes 3145728 | tf_op jit(solution)/shard_map/all_to_all | solution.py:90
  305.5 76.7 %psum.7 = f32[32]{0:T(128)S(1)} all-reduce(f32[32]{0:T(128)S(1)} %pad_maximum_fusion.4), channel_id=1, replica_groups=mesh['dp'=32,'tensor'=4] {'dp'}, use_global_device_ids=true, to_apply=%region_18.20 | all-reduce | flops 32 | bytes 256 | tf_op jit(solution)/shard_map/psum | solution.py:12
  382.9 1.2 convert_reduce_fusion
  384.0 1.2 reshape.143
  386.6 0.7 pad_maximum_fusion
  (60 shorter events, 7.3 us)
Async XLA Ops:
  7.2 103.1 %all-gather.5.cloned.1.call-start = ((), (), s32[]{:S(2)}) async-start(), calls=%async_computation.8 | async-start | bytes 7864320 | tf_op jit(solution)/shard_map/all_gather | solution.py:81
  13.0 1.3 copy-start.1
  13.0 1.5 copy-start
  47.2 131.0 %all-gather.3.cloned.1.call-start = ((), (), s32[]{:S(2)}) async-start(), calls=%async_computation.6 | async-start | bytes 7864320 | tf_op jit(solution)/shard_map/all_gather | solution.py:81
  74.2 162.6 %reduce-scatter.5.cloned.1.call-start = ((), (), s32[]{:S(2)}) async-start(), calls=%async_computation.9 | async-start | bytes 6553600 | tf_op jit(solution)/shard_map/reduce_scatter | solution.py:87
  148.6 145.7 %reduce-scatter.3.cloned.1.call-start = ((), (), s32[]{:S(2)}) async-start(), calls=%async_computation.7 | async-start | bytes 6553600 | tf_op jit(solution)/shard_map/reduce_scatter | solution.py:87
  240.0 57.5 %all-to-all-start.3 = ((bf16[32,20,1024]{2,1,0:T(8,128)(2,1)}), bf16[32,20,1024]{2,1,0:T(8,128)(2,1)S(1)}, u32[]{:S(2)}, u32[]{:S(2)}) async-start(bf16[32,20,1024]{2,1,0:T(8,128)(2,1)} %convert_element_type.98), calls=%async_computation.5 | async-start | bytes 3145728 | tf_op jit(solution)/shard_map/all_to_all | solution.py:90
  297.5 87.7 %all-to-all-start.1 = ((bf16[32,20,1024]{2,1,0:T(8,128)(2,1)}), bf16[32,20,1024]{2,1,0:T(8,128)(2,1)S(1)}, u32[]{:S(2)}, u32[]{:S(2)}) async-start(bf16[32,20,1024]{2,1,0:T(8,128)(2,1)} %convert_element_type.90), calls=%async_computation.2 | async-start | bytes 3145728 | tf_op jit(solution)/shard_map/all_to_all | solution.py:90
Sparse Core Ops, SparseCore 0:
  47.3 62.8 all-gather.4
  111.9 66.2 all-gather.2
  180.6 56.1 reduce-scatter.4
  239.1 55.1 reduce-scatter.2
where the time goes:
time: 395 us; the launch traced here: 394 us
  blocking collectives  135 us (34%)
  waiting for transfers between devices  132 us (33%)
  matrix products  62.5 us (16%)
  local copies, waits for them, and re-layouts  28.3 us (7%)
  starting transfers between devices  15.8 us (4%)
  between operations  14 us (4%)
  other arithmetic  5.56 us (1%)
    psum x1, blocking collectives, together(): subtotal = lax.psum(ravelled, axis)  76.7 us
    reduce_scatter x2, waiting for transfers between devices, local(): lax.psum_scatter(part, 'tensor', scatter_dimension=1, tiled=True)  67 us
    all_gather x2, waiting for transfers between devices, local(): piece = lax.all_gather(arrived, 'tensor', axis=2, tiled=True)  65.4 us
    all_to_all x2, blocking collectives, local(): lax.all_to_all(spread_slots(slots, experts, copies_per, capacity), 'dp',...  58.5 us
    dot_general x2, matrix products, local(): jnp.dot(hidden, down_local, preferred_element_type=jnp.float32)  37.8 us
    dot_general x2, matrix products, local(): gate = jnp.dot(piece_rows, gate_local, preferred_element_type=jnp.float32)  23.2 us
    all_to_all x2, starting transfers between devices, local(): lax.all_to_all(reduced.reshape(groups, capacity, width_local).astype(jnp....  15.4 us
    reshape x2, local copies, waits for them, and re-layouts, local(): piece_rows = piece.reshape(-1, piece.shape[2])  15.4 us
  transfers between devices with their start and end apart: 6, of which 4 were waited for; matrix products, arithmetic and copies ran while one was open for 22% of the time, Pallas kernels for 0%

commit v1 on v0

--- a/solution.py
+++ b/solution.py
@@ -78,7 +78,8 @@
             concat_axis=0,
             tiled=True,
         )
-        piece = lax.all_gather(arrived, "tensor", axis=2, tiled=True)
+        blocks = lax.all_gather(arrived, "tensor")
+        piece = jnp.concatenate(blocks, axis=2)
         piece_rows = piece.reshape(-1, piece.shape[2])
         gate = jnp.dot(piece_rows, gate_local, preferred_element_type=jnp.float32)
         up = jnp.dot(piece_rows, up_local, preferred_element_type=jnp.float32)

time: 395 us -> 383 us (0.970)
  waiting for transfers between devices: 132 us -> 101 us
  local copies, waits for them, and re-layouts: 28.3 us -> 41.8 us
    all_gather x2, waiting for transfers between devices: 65.4 us -> 35.1 us  [local(): blocks = lax.all_gather(arrived, 'tensor')]
    unnamed x4 -> x18, local copies, waits for them, and re-layouts: 0.01 us -> 11.9 us
    dot_general x2, matrix products: 37.8 us -> 48.9 us  [local(): jnp.dot(hidden, down_local, preferred_element_type=jnp.float32)]
    dot_general x2, matrix products: 23.2 us -> 13.8 us  [local(): gate = jnp.dot(piece_rows, gate_local, preferred_element_type=jnp.float32)]
  transfers between devices with their start and end apart: 6 -> 6, of which waited for: 4 -> 4; matrix products, arithmetic and copies ran while one was open for 22% -> 25% of each run, Pallas kernels for 0% -> 0%
where the time goes in v1:
time: 383 us; the launch traced here: 378 us
  blocking collectives  135 us (35%)
  waiting for transfers between devices  101 us (26%)
  matrix products  64.2 us (17%)
  local copies, waits for them, and re-layouts  41.8 us (11%)
  starting transfers between devices  16 us (4%)
  between operations  14.3 us (4%)
  other arithmetic  5.54 us (1%)
    psum x1, blocking collectives, together(): subtotal = lax.psum(ravelled, axis)  76.7 us
    reduce_scatter x2, waiting for transfers between devices, local(): lax.psum_scatter(part, 'tensor', scatter_dimension=1, tiled=True)  66 us
    all_to_all x2, blocking collectives, local(): lax.all_to_all(spread_slots(slots, experts, copies_per, capacity), 'dp',...  58.3 us
    dot_general x2, matrix products, local(): jnp.dot(hidden, down_local, preferred_element_type=jnp.float32)  48.9 us
    all_gather x2, waiting for transfers between devices, local(): blocks = lax.all_gather(arrived, 'tensor')  35.1 us
    all_to_all x2, starting transfers between devices, local(): lax.all_to_all(reduced.reshape(groups, capacity, width_local).astype(jnp....  15.5 us
    dot_general x2, matrix products, local(): gate = jnp.dot(piece_rows, gate_local, preferred_element_type=jnp.float32)  13.8 us
    reshape x2, local copies, waits for them, and re-layouts, local(): piece = jnp.concatenate(blocks, axis=2)  13.4 us
  transfers between devices with their start and end apart: 6, of which 4 were waited for; matrix products, arithmetic and copies ran while one was open for 25% of the time, Pallas kernels for 0%

profile of v1, /device:TPU:1, one launch (start us, length us, event | category | flops | bytes accessed | tf_op | source)
XLA Modules:
  0.0 378.0 jit_solution(11702474386999660970)
XLA Ops:
  15.0 32.0 %all_to_all.20 = bf16[32,20,1024]{2,1,0:T(8,128)(2,1)S(1)} all-to-all(bf16[32,20,1024]{2,1,0:T(8,128)(2,1)S(1)} %bitcast.111), channel_id=1, replica_groups=mesh['dp'=32,'tensor'=4] {'dp'}, dimensions={0} | all-to-all | bytes 2621440 | tf_op jit(solution)/shard_map/all_to_all | solution.py:74
  47.1 1.8 copy.74
  49.5 26.3 %all_to_all.21 = bf16[32,20,1024]{2,1,0:T(8,128)(2,1)S(1)} all-to-all(bf16[32,20,1024]{2,1,0:T(8,128)(2,1)S(1)} %bitcast.112), channel_id=1, replica_groups=mesh['dp'=32,'tensor'=4] {'dp'}, dimensions={0} | all-to-all | bytes 2621440 | tf_op jit(solution)/shard_map/all_to_all | solution.py:74
  75.7 1.8 copy.68
  78.0 25.2 %all-gather.7.cloned.1.call-done = bf16[128,20,1024]{2,0,1:T(8,128)(2,1)} async-done(((bf16[32,20,1024]{2,0,1:T(8,128)(2,1)}), bf16[128,20,1024]{2,0,1:T(8,128)(2,1)}) %all-gather.7.cloned.1.call-update) | async-done | bytes 5242896 | tf_op jit(solution)/shard_map/all_gather | solution.py:81
  103.2 6.7 %copy.75 = bf16[32,20,4,1024]{3,2,1,0:T(4,128)(2,1)S(1)} copy(bf16[32,20,4,1024]{3,0,2,1:T(8,128)(2,1)} %bitcast.114) | data formatting | bytes 10485760 | tf_op jit(solution)/shard_map/reshape | solution.py:82
  109.9 3.5 copy.77
  113.4 2.4 copy-done
  115.8 6.9 %fusion.8 = f32[640,896]{1,0:T(8,128)} fusion(bf16[640,4096]{1,0:T(8,128)(2,1)S(1)} %bitcast.115, bf16[1,4096,896]{2,1,0:T(8,128)(2,1)S(1)} %bitcast.122), kind=kOutput, calls=%fused_computation.10 | convolution fusion | flops 4697620480 | bytes 14876672 | tf_op jit(solution)/shard_map/dot_general | solution.py:84
  122.7 29.6 %fusion.15 = bf16[640,4096]{1,0:T(8,128)(2,1)} fusion(bf16[1,896,4096]{2,1,0:T(8,128)(2,1)} %param.13, f32[640,896]{1,0:T(8,128)} %fusion.8, bf16[640,4096]{1,0:T(8,128)(2,1)} %bitcast.116, bf16[1,4096,896]{2,1,0:T(8,128)(2,1)} %param.12), kind=kOutput, calls=%fused_computation.15 | convolution fusion | flops 9401303040 | bytes 27459584 | tf_op jit(solution)/shard_map/dot_general | solution.py:87
  152.4 9.9 %all-gather.5.cloned.1.call-done = bf16[128,20,1024]{2,0,1:T(8,128)(2,1)} async-done(((bf16[32,20,1024]{2,0,1:T(8,128)(2,1)}), bf16[128,20,1024]{2,0,1:T(8,128)(2,1)}) %all-gather.5.cloned.1.call-update) | async-done | bytes 5242896 | tf_op jit(solution)/shard_map/all_gather | solution.py:81
  162.3 6.7 %copy.69 = bf16[32,20,4,1024]{3,2,1,0:T(4,128)(2,1)S(1)} copy(bf16[32,20,4,1024]{3,0,2,1:T(8,128)(2,1)} %bitcast.113) | data formatting | bytes 10485760 | tf_op jit(solution)/shard_map/reshape | solution.py:82
  169.0 3.5 copy.76
  172.5 2.6 copy-done.1
  175.1 6.9 %fusion.10 = f32[640,896]{1,0:T(8,128)} fusion(bf16[640,4096]{1,0:T(8,128)(2,1)S(1)} %bitcast.117, bf16[1,4096,896]{2,1,0:T(8,128)(2,1)S(1)} %bitcast.124), kind=kOutput, calls=%fused_computation.12 | convolution fusion | flops 4697620480 | bytes 14876672 | tf_op jit(solution)/shard_map/dot_general | solution.py:84
  182.0 19.2 %fusion.12 = bf16[640,4096]{1,0:T(8,128)(2,1)} fusion(bf16[1,896,4096]{2,1,0:T(8,128)(2,1)} %param.13, f32[640,896]{1,0:T(8,128)} %fusion.10, bf16[640,4096]{1,0:T(8,128)(2,1)} %bitcast.118, bf16[1,4096,896]{2,1,0:T(8,128)(2,1)} %param.12), kind=kOutput, calls=%fused_computation.14 | convolution fusion | flops 9401303040 | bytes 27459584 | tf_op jit(solution)/shard_map/dot_general | solution.py:87
  201.3 19.5 %reduce-scatter.5.cloned.1.call-done = bf16[640,1024]{1,0:T(8,128)(2,1)} async-done(((bf16[640,4096]{1,0:T(8,128)(2,1)}), bf16[640,1024]{1,0:T(8,128)(2,1)}) %reduce-scatter.5.cloned.1.call-update) | async-done | bytes 1310736 | tf_op jit(solution)/shard_map/reduce_scatter | solution.py:88
  220.8 3.2 convert_element_type.98
  224.0 7.8 %all-to-all-start.3 = ((bf16[32,20,1024]{2,1,0:T(8,128)(2,1)}), bf16[32,20,1024]{2,1,0:T(8,128)(2,1)S(1)}, u32[]{:S(2)}, u32[]{:S(2)}) async-start(bf16[32,20,1024]{2,1,0:T(8,128)(2,1)} %convert_element_type.98), calls=%async_computation.5 | async-start | bytes 3145728 | tf_op jit(solution)/shard_map/all_to_all | solution.py:91
  231.7 46.5 %reduce-scatter.3.cloned.1.call-done = bf16[640,1024]{1,0:T(8,128)(2,1)} async-done(((bf16[640,4096]{1,0:T(8,128)(2,1)}), bf16[640,1024]{1,0:T(8,128)(2,1)}) %reduce-scatter.3.cloned.1.call-update) | async-done | bytes 1310736 | tf_op jit(solution)/shard_map/reduce_scatter | solution.py:88
  278.2 3.2 convert_element_type.90
  281.4 7.7 %all-to-all-start.1 = ((bf16[32,20,1024]{2,1,0:T(8,128)(2,1)}), bf16[32,20,1024]{2,1,0:T(8,128)(2,1)S(1)}, u32[]{:S(2)}, u32[]{:S(2)}) async-start(bf16[32,20,1024]{2,1,0:T(8,128)(2,1)} %convert_element_type.90), calls=%async_computation.2 | async-start | bytes 3145728 | tf_op jit(solution)/shard_map/all_to_all | solution.py:91
  289.5 76.7 %psum.7 = f32[32]{0:T(128)S(1)} all-reduce(f32[32]{0:T(128)S(1)} %pad_maximum_fusion.4), channel_id=1, replica_groups=mesh['dp'=32,'tensor'=4] {'dp'}, use_global_device_ids=true, to_apply=%region_18.20 | all-reduce | flops 32 | bytes 256 | tf_op jit(solution)/shard_map/psum | solution.py:12
  368.0 1.2 reshape.143
  (78 shorter events, 13.0 us)
Async XLA Ops:
  7.2 96.1 %all-gather.7.cloned.1.call-start = ((), (), s32[]{:S(2)}) async-start(), calls=%async_computation.9 | async-start | bytes 6553600 | tf_op jit(solution)/shard_map/all_gather | solution.py:81
  13.0 1.3 copy-start.3
  13.0 1.5 copy-start.2
  48.9 113.4 %all-gather.5.cloned.1.call-start = ((), (), s32[]{:S(2)}) async-start(), calls=%async_computation.8 | async-start | bytes 6553600 | tf_op jit(solution)/shard_map/all_gather | solution.py:81
  77.6 143.2 %reduce-scatter.5.cloned.1.call-start = ((), (), s32[]{:S(2)}) async-start(), calls=%async_computation.7 | async-start | bytes 6553600 | tf_op jit(solution)/shard_map/reduce_scatter | solution.py:88
  103.2 12.5 %slice-start = ((s8[7340032]{0:T(1024)(128)(4,1)}), s8[4194304]{0:T(1024)(128)(4,1)S(1)}, s32[]{:S(2)}) async-start(s8[7340032]{0:T(1024)(128)(4,1)} %bitcast.121), calls=%async_computation.10 | async-start | bytes 8388608
  109.9 5.9 %slice-start.1 = ((s8[7340032]{0:T(1024)(128)(4,1)}), s8[3145728]{0:T(1024)(128)(4,1)S(1)}, s32[]{:S(2)}) async-start(s8[7340032]{0:T(1024)(128)(4,1)} %bitcast.121), calls=%async_computation.11 | async-start | bytes 6291456
  113.4 2.4 copy-start
  152.4 125.9 %reduce-scatter.3.cloned.1.call-start = ((), (), s32[]{:S(2)}) async-start(), calls=%async_computation.6 | async-start | bytes 6553600 | tf_op jit(solution)/shard_map/reduce_scatter | solution.py:88
  162.3 12.8 %slice-start.2 = ((s8[7340032]{0:T(1024)(128)(4,1)}), s8[4194304]{0:T(1024)(128)(4,1)S(1)}, s32[]{:S(2)}) async-start(s8[7340032]{0:T(1024)(128)(4,1)} %bitcast.123), calls=%async_computation.12 | async-start | bytes 8388608
  169.0 6.1 %slice-start.3 = ((s8[7340032]{0:T(1024)(128)(4,1)}), s8[3145728]{0:T(1024)(128)(4,1)S(1)}, s32[]{:S(2)}) async-start(s8[7340032]{0:T(1024)(128)(4,1)} %bitcast.123), calls=%async_computation.13 | async-start | bytes 6291456
  172.5 2.6 copy-start.1
  224.0 57.5 %all-to-all-start.3 = ((bf16[32,20,1024]{2,1,0:T(8,128)(2,1)}), bf16[32,20,1024]{2,1,0:T(8,128)(2,1)S(1)}, u32[]{:S(2)}, u32[]{:S(2)}) async-start(bf16[32,20,1024]{2,1,0:T(8,128)(2,1)} %convert_element_type.98), calls=%async_computation.5 | async-start | bytes 3145728 | tf_op jit(solution)/shard_map/all_to_all | solution.py:91
  281.4 87.7 %all-to-all-start.1 = ((bf16[32,20,1024]{2,1,0:T(8,128)(2,1)}), bf16[32,20,1024]{2,1,0:T(8,128)(2,1)S(1)}, u32[]{:S(2)}, u32[]{:S(2)}) async-start(bf16[32,20,1024]{2,1,0:T(8,128)(2,1)} %convert_element_type.90), calls=%async_computation.2 | async-start | bytes 3145728 | tf_op jit(solution)/shard_map/all_to_all | solution.py:91
Sparse Core Ops, SparseCore 0:
  49.0 54.1 all-gather.6
  104.9 57.3 all-gather.4
  164.7 55.9 reduce-scatter.4
  223.0 55.1 reduce-scatter.2
